TPU v7x, 32 devices: a whole 2x2x4 slice. The times are simulated.
32 devices in a mesh: dp: 4 (over x, y), tp: 8 (over z, core).
Axes of the slice: x: 2, y: 2, z: 4, core: 2. Of those that a mesh axis runs over, the one named last changes fastest.
Arguments:
- x: bfloat16 [7168, 5120], P(('dp', 'tp')), parts along dimension 0
- dy: bfloat16 [7168, 5120], P(('dp', 'tp')), parts along dimension 0
- gate: bfloat16 [7168, 16384], P('dp', 'tp'), parts along dimension 0
- up: bfloat16 [7168, 16384], P('dp', 'tp'), parts along dimension 0
- w_gate: bfloat16 [5120, 16384], P(None, 'tp')
- w_up: bfloat16 [5120, 16384], P(None, 'tp')
- w_down: bfloat16 [16384, 5120], P('tp')
Outputs:
- output 1: bfloat16 [7168, 5120], P(('dp', 'tp')), parts along dimension 0
- output 2: bfloat16 [20480, 16384], P('dp', 'tp'), parts along dimension 0
- output 3: bfloat16 [20480, 16384], P('dp', 'tp'), parts along dimension 0
- output 4: bfloat16 [65536, 5120], P(('dp', 'tp')), parts along dimension 0
There are 4 independent parts. A program takes and returns all parts, laid end to end along the dimension named above; an argument that names none is the same for every part.
All inputs are finite; a program needn't handle non-finite values.
Results may differ from a plain program's by a relative error of at most 0.012.
Values are sent between devices in bfloat16 or wider.
A program may use at most 2 GiB of HBM per device.

v0:
```python
import jax
import jax.numpy as jnp


def act(gate, up):
    return jax.nn.silu(gate) * up


def solution(mesh):
    def step(x, dy, gate, up, w_gate, w_up, w_down):
        hidden, back = jax.vjp(act, gate.astype(jnp.float32), up.astype(jnp.float32))
        d_hidden = jnp.dot(dy, w_down.T, preferred_element_type=jnp.float32)
        d_gate, d_up = (g.astype(jnp.bfloat16) for g in back(d_hidden))
        dx = jnp.dot(d_gate, w_gate.T) + jnp.dot(d_up, w_up.T)
        groups = mesh.shape["dp"]

        def by_group(a, b):
            a, b = (t.reshape(groups, -1, t.shape[-1]) for t in (a, b))
            product = jnp.einsum("gta,gtb->gab", a, b, preferred_element_type=jnp.float32)
            return product.astype(jnp.bfloat16).reshape(-1, b.shape[-1])

        return dx, by_group(x, d_gate), by_group(x, d_up), by_group(hidden.astype(jnp.bfloat16), dy)

    return step
```

profile of v0, /device:TPU:1, one launch (start us, length us, event | category | flops | bytes accessed | tf_op | source)
XLA Modules:
  0.0 789.8 jit_solution(12274384573163654228)
XLA Ops:
  7.2 0.0 all-gather.9.cloned.1.call-start
  7.2 3.2 copy.15
  10.4 0.0 all-gather.9.cloned.1.call-update
  10.4 0.0 all-gather.11.cloned.1.call-start
  10.5 0.7 all-gather.11.cloned.1.call-update
  11.2 0.0 reduce-scatter.4.cloned.1.call-start
  11.2 165.8 %all-gather.9.cloned.1.call-done = bf16[1792,5120]{1,0:T(8,128)(2,1)} async-done(((bf16[224,5120]{1,0:T(8,128)(2,1)}), bf16[1792,5120]{1,0:T(8,128)(2,1)}) %all-gather.9.cloned.1.call-update) | async-done | bytes 18350096 | tf_op args[1]
  177.1 48.6 %fusion.23 = f32[1792,2048]{1,0:T(8,128)} fusion(bf16[1792,5120]{1,0:T(8,128)(2,1)} %all-gather.9.cloned.1.call-done, bf16[2048,5120]{1,0:T(8,128)(2,1)} %param.3), kind=kOutput, calls=%fused_computation.40 | convolution fusion | flops 37580963840 | bytes 54001664 | tf_op jit(solution)/dot_general | solution.py:12
  225.6 15.1 %fusion.22 = (bf16[1,1792,2048]{2,1,0:T(8,128)(2,1)}, bf16[1792,2048]{1,0:T(8,128)(2,1)S(1)}) fusion(bf16[1792,2048]{1,0:T(8,128)(2,1)} %param.4, bf16[1792,2048]{1,0:T(8,128)(2,1)} %param.5, f32[1792,2048]{1,0:T(8,128)} %fusion.23), kind=kLoop, calls=%fused_computation.39 | loop fusion | flops 58720256 | bytes 44040192 | tf_op jit(solution)/reshape | solution.py:18
  240.8 0.0 copy-start
  240.8 3.0 copy-done
  243.8 44.6 %fusion.24 = bf16[1792,5120]{1,0:T(8,128)(2,1)} fusion(bf16[1792,2048]{1,0:T(8,128)(2,1)S(1)} %get-tuple-element.40, bf16[5120,2048]{1,0:T(8,128)(2,1)} %param.6), kind=kOutput, calls=%fused_computation.41 | convolution fusion | flops 37580963840 | bytes 46661632 | tf_op jit(solution)/dot_general | solution.py:14
  288.4 69.6 %convolution_add_fusion = bf16[1792,5120]{1,0:T(8,128)(2,1)} fusion(bf16[1792,5120]{1,0:T(8,128)(2,1)} %fusion.24, bf16[5120,2048]{1,0:T(8,128)(2,1)} %param.7, f32[1792,2048]{1,0:T(8,128)} %fusion.23, bf16[1792,2048]{1,0:T(8,128)(2,1)} %param.5), kind=kOutput, calls=%fused_computation.30 | convolution fusion | flops 37615828992 | bytes 79691776 | tf_op jit(solution)/dot_general | solution.py:14
  358.0 0.0 reduce-scatter.4.cloned.1.call-update
  358.0 0.1 collective-permute-start.4
  358.1 0.0 all-gather.11.cloned.1.call-done
  358.1 51.5 %convert_bitcast_fusion = bf16[5120,2048]{0,1:T(8,128)(2,1)} fusion(bf16[1792,5120]{1,0:T(8,128)(2,1)} %all-gather.11.cloned.1.call-done, f32[1792,2048]{1,0:T(8,128)} %fusion.23, bf16[1792,2048]{1,0:T(8,128)(2,1)} %param.5), kind=kOutput, calls=%fused_computation.25 | convolution fusion | flops 37617139712 | bytes 61341696 | tf_op jit(solution)/gta,gtb->gab/dot_general | solution.py:19
  409.6 45.9 %convert_bitcast_fusion.1 = bf16[5120,2048]{0,1:T(8,128)(2,1)} fusion(bf16[1792,2048]{1,0:T(8,128)(2,1)} %copy-done, bf16[1792,5120]{1,0:T(8,128)(2,1)} %all-gather.11.cloned.1.call-done), kind=kOutput, calls=%fused_computation.26 | convolution fusion | flops 37591449600 | bytes 46661632 | tf_op jit(solution)/gta,gtb->gab/dot_general | solution.py:19
  455.6 28.2 %copy = bf16[5120,2048]{1,0:T(8,128)(2,1)} copy(bf16[5120,2048]{0,1:T(8,128)(2,1)} %convert_bitcast_fusion.1) | data formatting | bytes 41943040
  483.8 0.0 copy-start.1
  483.8 28.2 %copy.1 = bf16[5120,2048]{1,0:T(8,128)(2,1)} copy(bf16[5120,2048]{0,1:T(8,128)(2,1)} %convert_bitcast_fusion) | data formatting | bytes 41943040
  512.0 0.0 collective-permute-done.4
  512.0 0.0 copy-done.1
  512.0 249.0 %while.2 = (bf16[1,1792,2048]{2,1,0:T(8,128)(2,1)}, bf16[1,1,224,5120]{3,2,1,0:T(8,128)(2,1)}, f32[1,2048,5120]{2,1,0:T(8,128)}, bf16[1,1,224,5120]{3,2,1,0:T(8,...) while((bf16[1,1792,2048]{2,1,0:T(8,128)(2,1)}, ...), condition=%wide.windowed_dot_general_cond_ag.clone, body=%wide.windowed_dot_general_body_ag.clone.sunk | while | flops 18833866752 | bytes 228328016 | solution.py:19
  512.3 0.5 collective-permute-start
  512.8 1.3 collective-permute-start.2
  514.1 0.6 dynamic-slice.65
  516.7 21.7 %fusion.39 = f32[2048,5120,1]{1,0,2:T(8,128)} fusion(bf16[1,1,224,5120]{3,2,1,0:T(8,128)(2,1)} %get-tuple-element.86, bf16[1,1,224,5120]{3,2,1,0:T(8,128)(2,1)} %get-tuple-element.84, s32[]{:T(128)S(6)} %multiply.15, bf16[1,1,1792,2048]{3,2,1,0:T(8,128)(2,1)} %bitcast.65, s32[]{:T(128)S(6)} %multiply.16), kind=kOutput, calls=%fused_computation.7.clone.1 | convolution fusion | flops 9401204736 | bytes 53870600 | tf_op jit(solution)/gta,gtb->gab/dot_general | solution.py:19
  538.3 68.0 %collective-permute-done = bf16[1,1,224,5120]{3,2,1,0:T(8,128)(2,1)S(1)} collective-permute-done((bf16[1,1,224,5120]{3,2,1,0:T(8,128)(2,1)}, bf16[1,1,224,5120]{3,2,1,0:T(8,128)(2,1)S(1)}, u32[]{:S(2)}, u32[]{:S(2)}) %collective-permute-start) | collective-permute-done | bytes 2293792 | tf_op jit(solution)/gta,gtb->gab/dot_general | solution.py:19
  606.3 0.0 collective-permute-start.1
  606.3 0.0 collective-permute-done.2
  606.3 1.7 collective-permute-start.3
  608.1 33.5 %bitcast_add_fusion.3 = f32[1,2048,5120]{2,1,0:T(8,128)} fusion(f32[2048,5120,1]{1,0,2:T(8,128)} %fusion.39, f32[1,2048,5120]{2,1,0:T(8,128)} %get-tuple-element.85, pred[]{:T(512)S(6)} %compare.6, bf16[1,1,224,5120]{3,2,1,0:T(8,128)(2,1)} %collective-permute-done.2, bf16[1,1,224,5120]{3,2,1,0:T(8,128)(2,1)S(1)} %collective-permute-done, ...), kind=kOutput, calls=%fused_computation.clone.1 | convolution fusion | flops 9432662016 | bytes 137756688 | tf_op jit(solution)/gta,gtb->gab/dot_general | solution.py:19
  641.6 13.7 %collective-permute-done.1 = bf16[1,1,224,5120]{3,2,1,0:T(8,128)(2,1)} collective-permute-done((bf16[1,1,224,5120]{3,2,1,0:T(8,128)(2,1)S(1)}, bf16[1,1,224,5120]{3,2,1,0:T(8,128)(2,1)}, u32[]{:S(2)}, u32[]{:S(2)}) %collective-permute-start.1) | collective-permute-done | bytes 2293792 | tf_op jit(solution)/gta,gtb->gab/dot_general | solution.py:19
  655.2 1.9 collective-permute-done.3
  657.2 2.6 collective-permute-start
  659.8 0.0 collective-permute-start.2
  659.8 0.6 dynamic-slice.65
  662.3 21.7 %fusion.39 = f32[2048,5120,1]{1,0,2:T(8,128)} fusion(bf16[1,1,224,5120]{3,2,1,0:T(8,128)(2,1)} %get-tuple-element.86, bf16[1,1,224,5120]{3,2,1,0:T(8,128)(2,1)} %get-tuple-element.84, s32[]{:T(128)S(6)} %multiply.15, bf16[1,1,1792,2048]{3,2,1,0:T(8,128)(2,1)} %bitcast.65, s32[]{:T(128)S(6)} %multiply.16), kind=kOutput, calls=%fused_computation.7.clone.1 | convolution fusion | flops 9401204736 | bytes 53870600 | tf_op jit(solution)/gta,gtb->gab/dot_general | solution.py:19
  684.0 24.8 %collective-permute-done = bf16[1,1,224,5120]{3,2,1,0:T(8,128)(2,1)S(1)} collective-permute-done((bf16[1,1,224,5120]{3,2,1,0:T(8,128)(2,1)}, bf16[1,1,224,5120]{3,2,1,0:T(8,128)(2,1)S(1)}, u32[]{:S(2)}, u32[]{:S(2)}) %collective-permute-start) | collective-permute-done | bytes 2293792 | tf_op jit(solution)/gta,gtb->gab/dot_general | solution.py:19
  708.8 1.0 collective-permute-start.1
  709.8 0.0 collective-permute-done.2
  709.8 0.7 collective-permute-start.3
  710.5 44.1 %bitcast_add_fusion.3 = f32[1,2048,5120]{2,1,0:T(8,128)} fusion(f32[2048,5120,1]{1,0,2:T(8,128)} %fusion.39, f32[1,2048,5120]{2,1,0:T(8,128)} %get-tuple-element.85, pred[]{:T(512)S(6)} %compare.6, bf16[1,1,224,5120]{3,2,1,0:T(8,128)(2,1)} %collective-permute-done.2, bf16[1,1,224,5120]{3,2,1,0:T(8,128)(2,1)S(1)} %collective-permute-done, ...), kind=kOutput, calls=%fused_computation.clone.1 | convolution fusion | flops 9432662016 | bytes 137756688 | tf_op jit(solution)/gta,gtb->gab/dot_general | solution.py:19
  754.6 6.4 collective-permute-done.1
  761.0 0.0 collective-permute-done.3
  761.0 21.8 %convert_bitcast_fusion.2 = bf16[2048,5120]{1,0:T(8,128)(2,1)} fusion(f32[1,2048,5120]{2,1,0:T(8,128)} %get-tuple-element.6), kind=kLoop, calls=%fused_computation.27 | loop fusion | flops 10485760 | bytes 62914560 | tf_op jit(solution)/reshape | solution.py:20
  782.8 0.0 reduce-scatter.4.cloned.1.call-done
  (1 shorter events, 0.0 us)
Async XLA Ops:
  7.2 169.9 %all-gather.9.cloned.1.call-start = ((), (), s32[]{:S(2)}) async-start(), calls=%async_computation.1 | async-start | bytes 20643840 | tf_op args[1]
  10.4 347.7 %all-gather.11.cloned.1.call-start = ((), (), s32[]{:S(2)}) async-start(), calls=%async_computation.2 | async-start | bytes 20643840 | tf_op jit(solution)/reshape | solution.py:18
  11.2 771.6 %reduce-scatter.4.cloned.1.call-start = ((), (), s32[]{:S(2)}) async-start(), calls=%async_computation.3 | async-start | bytes 20643840
  240.8 3.0 copy-start
  358.0 154.0 %collective-permute-start.4 = (bf16[1,1,224,5120]{3,2,1,0:T(8,128)(2,1)}, bf16[1,1,224,5120]{3,2,1,0:T(8,128)(2,1)}, u32[]{:S(2)}, u32[]{:S(2)}) collective-permute-start(bf16[1,1,224,5120]{3,2,1,0:T(8,128)(2,1)} %bitcast.8), channel_id=9, source_target_pairs={{0,1},{1,2},{2,3},{3,4},{4,5},{5,6},{6,7},{7,0},{8,9},{9,10},{10,1... | collective-permute-start | bytes 6881288 | tf_op jit(solution)/gta,gtb->gab/dot_general | solution.py:19
  483.8 28.3 %copy-start.1 = (u32[32]{0:T(128)S(1)}, u32[32]{0:T(128)}, u32[]{:S(2)}) copy-start(u32[32]{0:T(128)} %constant.146) | copy-start | bytes 388
  512.3 94.0 %collective-permute-start = (bf16[1,1,224,5120]{3,2,1,0:T(8,128)(2,1)}, bf16[1,1,224,5120]{3,2,1,0:T(8,128)(2,1)S(1)}, u32[]{:S(2)}, u32[]{:S(2)}) collective-permute-start(bf16[1,1,224,5120]{3,2,1,0:T(8,128)(2,1)} %get-tuple-element.84), channel_id=10, source_target_pairs={{0,7},{1,0},{2,1},{3,2},{4,3},{5,4},{6,5},{7,6},{8,15},{9,8},{10,9... | collective-permute-start | bytes 6881288 | tf_op jit(solution)/gta,gtb->gab/dot_general | solution.py:19
  512.8 93.6 %collective-permute-start.2 = (bf16[1,1,224,5120]{3,2,1,0:T(8,128)(2,1)}, bf16[1,1,224,5120]{3,2,1,0:T(8,128)(2,1)}, u32[]{:S(2)}, u32[]{:S(2)}) collective-permute-start(bf16[1,1,224,5120]{3,2,1,0:T(8,128)(2,1)} %get-tuple-element.86), channel_id=11, source_target_pairs={{0,1},{1,2},{2,3},{3,4},{4,5},{5,6},{6,7},{7,0},{8,9},{9,10},{10,1... | collective-permute-start | bytes 6881288 | tf_op jit(solution)/gta,gtb->gab/dot_general | solution.py:19
  606.3 48.9 %collective-permute-start.1 = (bf16[1,1,224,5120]{3,2,1,0:T(8,128)(2,1)S(1)}, bf16[1,1,224,5120]{3,2,1,0:T(8,128)(2,1)}, u32[]{:S(2)}, u32[]{:S(2)}) collective-permute-start(bf16[1,1,224,5120]{3,2,1,0:T(8,128)(2,1)S(1)} %collective-permute-done), channel_id=12, source_target_pairs={{0,7},{1,0},{2,1},{3,2},{4,3},{5,4},{6,5},{7,6},{8,15},{9,8},{10,9... | collective-permute-start | bytes 6881288 | tf_op jit(solution)/gta,gtb->gab/dot_general | solution.py:19
  606.3 50.8 %collective-permute-start.3 = (bf16[1,1,224,5120]{3,2,1,0:T(8,128)(2,1)}, bf16[1,1,224,5120]{3,2,1,0:T(8,128)(2,1)}, u32[]{:S(2)}, u32[]{:S(2)}) collective-permute-start(bf16[1,1,224,5120]{3,2,1,0:T(8,128)(2,1)} %collective-permute-done.2), channel_id=13, source_target_pairs={{0,1},{1,2},{2,3},{3,4},{4,5},{5,6},{6,7},{7,0},{8,9},{9,10},{10,1... | collective-permute-start | bytes 6881288 | tf_op jit(solution)/gta,gtb->gab/dot_general | solution.py:19
  657.2 51.6 %collective-permute-start = (bf16[1,1,224,5120]{3,2,1,0:T(8,128)(2,1)}, bf16[1,1,224,5120]{3,2,1,0:T(8,128)(2,1)S(1)}, u32[]{:S(2)}, u32[]{:S(2)}) collective-permute-start(bf16[1,1,224,5120]{3,2,1,0:T(8,128)(2,1)} %get-tuple-element.84), channel_id=10, source_target_pairs={{0,7},{1,0},{2,1},{3,2},{4,3},{5,4},{6,5},{7,6},{8,15},{9,8},{10,9... | collective-permute-start | bytes 6881288 | tf_op jit(solution)/gta,gtb->gab/dot_general | solution.py:19
  659.8 50.1 %collective-permute-start.2 = (bf16[1,1,224,5120]{3,2,1,0:T(8,128)(2,1)}, bf16[1,1,224,5120]{3,2,1,0:T(8,128)(2,1)}, u32[]{:S(2)}, u32[]{:S(2)}) collective-permute-start(bf16[1,1,224,5120]{3,2,1,0:T(8,128)(2,1)} %get-tuple-element.86), channel_id=11, source_target_pairs={{0,1},{1,2},{2,3},{3,4},{4,5},{5,6},{6,7},{7,0},{8,9},{9,10},{10,1... | collective-permute-start | bytes 6881288 | tf_op jit(solution)/gta,gtb->gab/dot_general | solution.py:19
  708.8 52.2 %collective-permute-start.1 = (bf16[1,1,224,5120]{3,2,1,0:T(8,128)(2,1)S(1)}, bf16[1,1,224,5120]{3,2,1,0:T(8,128)(2,1)}, u32[]{:S(2)}, u32[]{:S(2)}) collective-permute-start(bf16[1,1,224,5120]{3,2,1,0:T(8,128)(2,1)S(1)} %collective-permute-done), channel_id=12, source_target_pairs={{0,7},{1,0},{2,1},{3,2},{4,3},{5,4},{6,5},{7,6},{8,15},{9,8},{10,9... | collective-permute-start | bytes 6881288 | tf_op jit(solution)/gta,gtb->gab/dot_general | solution.py:19
  709.8 51.2 %collective-permute-start.3 = (bf16[1,1,224,5120]{3,2,1,0:T(8,128)(2,1)}, bf16[1,1,224,5120]{3,2,1,0:T(8,128)(2,1)}, u32[]{:S(2)}, u32[]{:S(2)}) collective-permute-start(bf16[1,1,224,5120]{3,2,1,0:T(8,128)(2,1)} %collective-permute-done.2), channel_id=13, source_target_pairs={{0,1},{1,2},{2,3},{3,4},{4,5},{5,6},{6,7},{7,0},{8,9},{9,10},{10,1... | collective-permute-start | bytes 6881288 | tf_op jit(solution)/gta,gtb->gab/dot_general | solution.py:19
Sparse Core Ops, SparseCore 0:
  10.5 166.4 all-gather.8
  178.7 162.7 all-gather.10
  358.2 243.2 reduce-scatter.3
where the time goes:
time: 800 us; the launch traced here: 790 us
  matrix products  381 us (48%)
  waiting for transfers between devices  281 us (35%)
  local copies, waits for them, and re-layouts  63.9 us (8%)
  other arithmetic  36.9 us (5%)
  between operations  14.3 us (2%)
  starting transfers between devices  8.07 us (1%)
    dot_general x6, matrix products, by_group(): jnp.einsum('gta,gtb->gab', a, b, preferred_element_type=jnp.float32)  218 us
    unnamed x5, waiting for transfers between devices  167 us
    dot_general x9, waiting for transfers between devices, by_group(): jnp.einsum('gta,gtb->gab', a, b, preferred_element_type=jnp.float32)  115 us
    dot_general x2, matrix products, step(): dx = jnp.dot(d_gate, w_gate.T) + jnp.dot(d_up, w_up.T)  114 us
    unnamed x7, local copies, waits for them, and re-layouts  62.7 us
    dot_general x1, matrix products, step(): d_hidden = jnp.dot(dy, w_down.T, preferred_element_type=jnp.float32)  48.6 us
    reshape x1, other arithmetic, by_group(): return product.astype(jnp.bfloat16).reshape(-1, b.shape[-1])  21.8 us
  transfers between devices with their start and end apart: 12, of which 6 were waited for; matrix products, arithmetic and copies ran while one was open for 60% of the time, Pallas kernels for 0%

commit v1 on v0

v1 whole, which is shorter than its diff:
```python
import jax
import jax.numpy as jnp
from jax import lax
from jax.experimental import pallas as pl
from jax.experimental.pallas import tpu as pltpu
from jax.sharding import PartitionSpec as P

BF = jnp.bfloat16
F32 = jnp.float32
MESH = pl.DeviceIdType.MESH

R = 224
D = 5120
F = 2048
H = 2
HR = R // H
Q = 5
QC = D // Q
NH = 256
ND = 512
K2 = D // 2


def dot(a, b, ca, cb):
    return lax.dot_general(a, b, (((ca,), (cb,)), ((), ())), preferred_element_type=F32)


def kernel(
    x, dy, gate, up, w_gate, w_up, w_down,
    dx, dwg, dwu, dwd, dyg, xg, pown, psend, precv, rsend, rrecv,
    hid, dg, du, dyb, gub, wd, wgu, tile, ost, stf, stb, rsf,
    s_wd, s_wgu, s_gub, s_dyb, s_tile, s_out, s_st, s_rs,
    sd_r, sd_l, sd_p, rd, sx_r, sx_l, sx_p, rx, sp, rp, sr, rr,
):
    me = lax.axis_index("tp")
    z = me // 2
    c = lax.rem(me, 2)
    other = me + 1 - 2 * c
    right, left = me + 2, me - 2
    is_end = (z == 0) | (z == 3)
    is_mid = (z == 1) | (z == 2)
    zz = jnp.where(z < 2, z, 3 - z)

    def block_of(p):
        near = jnp.where((zz == 1) & (p < 2), 1 - p, p)
        return jnp.where(z < 2, near, 3 - near)

    def remote(src, dst, ssem, rsem, to):
        return pltpu.make_async_remote_copy(
            src_ref=src, dst_ref=dst, send_sem=ssem, recv_sem=rsem, device_id={"tp": to}, device_id_type=MESH
        )

    class Dy:
        own, all_, rs, ls, ps, rv, n = dy, dyg, sd_r, sd_l, sd_p, rd, H

        @staticmethod
        def own_at(i):
            return dy.at[pl.ds(i * HR, HR)]

        @staticmethod
        def at(blk, i):
            return dyg.at[blk, pl.ds(i * HR, HR)]

    class X:
        own, all_, rs, ls, ps, rv, n = x, xg, sx_r, sx_l, sx_p, rx, Q

        @staticmethod
        def own_at(i):
            return x.at[:, pl.ds(i * QC, QC)]

        @staticmethod
        def at(blk, i):
            return xg.at[blk, :, pl.ds(i * QC, QC)]

    def send_right(g, d, i, src):
        blk = me - 2 * d
        remote(src, g.at(blk, i), g.rs.at[d, i], g.rv.at[blk, i], right).start()

    def send_left(g, d, i, src):
        blk = me + 2 * d
        remote(src, g.at(blk, i), g.ls.at[d, i], g.rv.at[blk, i], left).start()

    def send_other(g, side, d, i, src):
        blk = me + (2 * d if side else -2 * d)
        remote(src, g.at(blk, i), g.ps.at[side, d, i], g.rv.at[blk, i], other).start()

    def wait_recv(g, blk, i):
        remote(g.at(blk, i), g.at(blk, i), g.ps.at[0, 0, i], g.rv.at[blk, i], other).wait_recv()

    def hop(g, d, i, gate_=True):
        @pl.when((z >= d) & gate_)
        def _():
            blk = me - 2 * d
            wait_recv(g, blk, i)

            @pl.when(z < 3)
            def _():
                send_right(g, d, i, g.at(blk, i))

            send_other(g, 0, d, i, g.at(blk, i))

        @pl.when((z + d <= 3) & gate_)
        def _():
            blk = me + 2 * d
            wait_recv(g, blk, i)

            @pl.when(z > 0)
            def _():
                send_left(g, d, i, g.at(blk, i))

            send_other(g, 1, d, i, g.at(blk, i))

    def wait_sends(g):
        def body(t, _):
            d, i = t // g.n, lax.rem(t, g.n)

            @pl.when((z < 3) & (d <= z))
            def _():
                remote(g.at(me, i), g.at(me, i), g.rs.at[d, i], g.rv.at[me, i], other).wait_send()

            @pl.when((z > 0) & (d <= 3 - z))
            def _():
                remote(g.at(me, i), g.at(me, i), g.ls.at[d, i], g.rv.at[me, i], other).wait_send()

            @pl.when(d <= z)
            def _():
                remote(g.at(me, i), g.at(me, i), g.ps.at[0, d, i], g.rv.at[me, i], other).wait_send()

            @pl.when((d > 0) & (d <= 3 - z))
            def _():
                remote(g.at(me, i), g.at(me, i), g.ps.at[1, d, i], g.rv.at[me, i], other).wait_send()

            return 0

        lax.fori_loop(0, 4 * g.n, body, 0)

    def x_step(s):
        @pl.when(s < Q)
        def _():
            send_other(X, 0, 0, s, X.own_at(s))

            @pl.when(is_mid)
            def _():
                send_right(X, 0, s, X.own_at(s))
                send_left(X, 0, s, X.own_at(s))

        @pl.when((s >= 1) & (s < Q + 1))
        def _():
            hop(X, 1, s - 1, is_mid)

        @pl.when((s >= 2) & (s < Q + 2))
        def _():
            hop(X, 2, s - 2, is_mid)

    def x_end(i):
        for d in (1, 2, 3):
            hop(X, d, i, is_end)

    def x_ready(i):
        for b in range(4):
            wait_recv(X, 2 * b + 1 - c, i)

    def wd_copy(n, slot):
        return pltpu.make_async_copy(w_down.at[pl.ds(n * NH, NH)], wd.at[slot], s_wd.at[slot])

    def wgu_copy(k, j, slot):
        src = w_up if k else w_gate
        return pltpu.make_async_copy(src.at[pl.ds(j * ND, ND)], wgu.at[slot, k], s_wgu.at[slot, k])

    def gub_copies(p):
        b = block_of(p)
        out = []
        for k, src in enumerate((gate, up)):
            for i, core in enumerate((c, 1 - c)):
                rows = pl.ds((2 * b + core) * R, R)
                out.append(pltpu.make_async_copy(src.at[rows], gub.at[k, pl.ds(i * R, R)], s_gub.at[k, i]))
        return out

    def dyb_copy(i, src):
        return pltpu.make_async_copy(src, dyb.at[pl.ds(i * R, R)], s_dyb.at[i])

    def tile_copies(own, all_, i, slot):
        cols = pl.ds(i * ND, ND)
        out = []
        for p in range(4):
            b = block_of(p)
            for k, core in enumerate((c, 1 - c)):
                src = own.at[:, cols] if p == 0 and k == 0 else all_.at[2 * b + core, :, cols]
                out.append(
                    pltpu.make_async_copy(src, tile.at[slot, pl.ds((2 * p + k) * R, R)], s_tile.at[slot, 2 * p + k])
                )
        return out

    def start(copies):
        for cp in copies:
            cp.start()

    def wait(copies):
        for cp in copies:
            cp.wait()

    def half(k):
        return pl.ds(pl.multiple_of(k * K2, K2), K2)

    def pair_send(p, k):
        return remote(psend.at[p, :, half(k)], precv.at[p, :, half(k)], sp.at[p, k], rp.at[p, k], other)

    def run_recv(t, k):
        return remote(rrecv.at[t, :, half(k)], rrecv.at[t, :, half(k)], sr.at[0, k], rr.at[t, k], other)

    def run_send(p, k, to, t):
        return remote(rsend.at[p, :, half(k)], rrecv.at[t, :, half(k)], sr.at[p, k], rr.at[t, k], to)

    def add_terms(p, k, extra, out):
        loads = [
            pltpu.make_async_copy(pown.at[p, :, half(k)], rsf, s_rs.at[0]),
            pltpu.make_async_copy(precv.at[p, :, half(k)], dyb.at[pl.ds(0, R), pl.ds(0, K2)], s_rs.at[1]),
        ]
        for n, t in enumerate(extra):
            loads.append(
                pltpu.make_async_copy(
                    rrecv.at[t, :, half(k)], dyb.at[pl.ds(R, R), pl.ds(n * K2, K2)], s_rs.at[2 + n]
                )
            )
        start(loads)
        wait(loads)

        def body(i, _):
            rows = pl.ds(pl.multiple_of(i * 32, 32), 32)
            low = pl.ds(pl.multiple_of(R + i * 32, 32), 32)
            v = rsf[rows] + dyb[rows, 0:K2].astype(F32)
            for n in range(len(extra)):
                v = v + dyb[low, n * K2 : (n + 1) * K2].astype(F32)
            dyb[rows, K2:D] = v.astype(BF)
            return 0

        lax.fori_loop(0, R // 32, body, 0)
        cp = pltpu.make_async_copy(dyb.at[pl.ds(0, R), pl.ds(K2, K2)], out, s_rs.at[4])
        cp.start()
        cp.wait()

    def pass_on(p, k, mid):
        t = block_of(p)
        pair_send(p, k).wait_recv()
        extra = ()
        if mid:
            run_recv(t, k).wait_recv()
            extra = (t,)
        add_terms(p, k, extra, rsend.at[p, :, half(k)])

        @pl.when(t > z)
        def _():
            run_send(p, k, right, t).start()

        @pl.when(t < z)
        def _():
            run_send(p, k, left, jnp.where(t == z - 1, 4, t)).start()

    def pass_on_both(p, mid):
        def body(k, _):
            pass_on(p, k, mid)
            return 0

        lax.fori_loop(0, 2, body, 0)

    barrier = pltpu.get_barrier_semaphore()

    def greet(to):
        pl.semaphore_signal(barrier, inc=1, device_id={"tp": to}, device_id_type=MESH)

    greet(other)

    @pl.when(z < 3)
    def _():
        greet(right)

    @pl.when(z > 0)
    def _():
        greet(left)

    for n in range(2):
        wd_copy(n, n).start()
    start(gub_copies(0))
    own_dyb = dyb_copy(0, dy)
    own_dyb.start()

    @pl.when(is_mid)
    def _():
        pl.semaphore_wait(barrier, 3)

    @pl.when(is_end)
    def _():
        pl.semaphore_wait(barrier, 2)

    for i in range(H):

        @pl.when(z < 3)
        def _():
            send_right(Dy, 0, i, Dy.own_at(i))

        @pl.when(z > 0)
        def _():
            send_left(Dy, 0, i, Dy.own_at(i))

        send_other(Dy, 0, 0, i, Dy.own_at(i))

    def end_x(i, _):
        @pl.when(z == 0)
        def _():
            send_right(X, 0, i, X.own_at(i))

        @pl.when(z == 3)
        def _():
            send_left(X, 0, i, X.own_at(i))

        return 0

    lax.fori_loop(0, Q, end_x, 0)
    for j in range(2):
        for k in range(2):
            wgu_copy(k, j, j).start()

    def phase(p, _):
        b = block_of(p)
        for i in range(H):
            wait_recv(Dy, 2 * b + 1 - c, i)
        theirs = dyb_copy(1, dyg.at[2 * b + 1 - c])
        theirs.start()

        @pl.when(p > 0)
        def _():
            dyb_copy(0, dyg.at[2 * b + c]).start()

        wait(gub_copies(p))
        own_dyb.wait()
        theirs.wait()
        rows = pl.ds(pl.multiple_of(p * 2 * R, 2 * R), 2 * R)

        def hidden_tile(n, _):
            slot = lax.rem(n, 2)
            cols = pl.ds(pl.multiple_of(n * NH, NH), NH)
            wd_copy(n, slot).wait()
            dh = dot(dyb[...], wd[slot], 1, 1)
            g = gub[0, :, cols].astype(F32)
            u = gub[1, :, cols].astype(F32)
            s = jax.nn.sigmoid(g)
            a = g * s
            hid[rows, cols] = (a * u).astype(BF)
            du[rows, cols] = (dh * a).astype(BF)
            dg[rows, cols] = (dh * (u * (s + a * (1.0 - s)))).astype(BF)

            @pl.when((n < F // NH - 2) | (p < 3))
            def _():
                wd_copy(lax.rem(n + 2, F // NH), slot).start()

            return 0

        lax.fori_loop(0, F // NH, hidden_tile, 0)

        @pl.when(p < 3)
        def _():
            start(gub_copies(p + 1))

        @pl.when(p < 3)
        def _():
            hop(Dy, p + 1, 0)

        @pl.when(p >= 2)
        def _():
            x_step(2 * p - 3)

            @pl.when(is_end)
            def _():
                pass_on_both(p - 1, False)

        def stage(j, slot):
            cols = pl.ds(pl.multiple_of(j * ND, ND), ND)
            return [
                pltpu.make_async_copy(stf.at[slot], pown.at[p, :, cols], s_st.at[0, slot]),
                pltpu.make_async_copy(stb.at[slot], psend.at[p, :, cols], s_st.at[1, slot]),
            ]

        def dx_tile(j, _):
            slot = lax.rem(j, 2)
            for k in range(2):
                wgu_copy(k, j, slot).wait()
            acc = dot(dg[rows, :], wgu[slot, 0], 1, 1) + dot(du[rows, :], wgu[slot, 1], 1, 1)

            @pl.when(j >= 2)
            def _():
                wait(stage(j - 2, slot))

            stf[slot] = acc[:R]
            stb[slot] = acc[R:].astype(BF)
            start(stage(j, slot))

            @pl.when((j < D // ND - 2) | (p < 3))
            def _():
                for k in range(2):
                    wgu_copy(k, lax.rem(j + 2, D // ND), slot).start()

            @pl.when(j == D // ND // 2 + 1)
            def _():
                pair_send(p, 0).start()

            return 0

        lax.fori_loop(0, D // ND, dx_tile, 0)
        for j in (D // ND - 2, D // ND - 1):
            wait(stage(j, j % 2))
        pair_send(p, 1).start()

        @pl.when(p < 3)
        def _():
            hop(Dy, p + 1, 1)

        @pl.when(p >= 1)
        def _():
            x_step(2 * p - 2)

        return 0

    lax.fori_loop(0, 4, phase, 0)

    def out_d(i, slot):
        cols = pl.ds(pl.multiple_of(i * ND, ND), ND)
        return pltpu.make_async_copy(ost.at[slot], dwd.at[:, cols], s_out.at[slot, 0])

    start(tile_copies(dy, dyg, 0, 0))

    def down_tile(i, _):
        slot = lax.rem(i, 2)

        @pl.when(i < D // ND - 1)
        def _():
            start(tile_copies(dy, dyg, i + 1, 1 - slot))

        @pl.when((i == 0) & is_end)
        def _():
            pass_on_both(3, False)

        @pl.when((i == 2) | (i == 4))
        def _():
            x_step(4 + i // 2)

        @pl.when(i == 7)
        def _():
            x_end(0)

        wait(tile_copies(dy, dyg, i, slot))

        @pl.when(i >= 2)
        def _():
            out_d(i - 2, slot).wait()

        for m in range(F // ND):
            ost[slot, m * ND : (m + 1) * ND, :] = dot(hid[:, m * ND : (m + 1) * ND], tile[slot], 0, 0).astype(BF)
        out_d(i, slot).start()
        return 0

    lax.fori_loop(0, D // ND, down_tile, 0)
    x_ready(0)
    start(tile_copies(x, xg, 0, 0))
    for i in (D // ND - 2, D // ND - 1):
        out_d(i, i % 2).wait()

    def out_gu(i, slot):
        rows = pl.ds(pl.multiple_of(i * ND, ND), ND)
        return [
            pltpu.make_async_copy(wgu.at[slot, k], (dwg, dwu)[k].at[rows], s_out.at[slot, k]) for k in range(2)
        ]

    def gu_tile(i, _):
        slot = lax.rem(i, 2)
        q = i // 2

        @pl.when((slot == 0) & (q < Q - 1))
        def _():
            x_end(q + 1)

        @pl.when((slot == 1) & (q < Q - 1))
        def _():
            x_ready(q + 1)

        @pl.when(i < D // ND - 1)
        def _():
            start(tile_copies(x, xg, i + 1, 1 - slot))

        @pl.when(is_mid & ((i == 2) | (i == 4)))
        def _():
            pass_on(3, i // 2 - 1, True)

        @pl.when(is_mid & (i == 5))
        def _():
            pass_on_both(2, True)

        @pl.when(is_mid & ((i == 6) | (i == 8)))
        def _():
            pass_on(1, i // 2 - 3, True)

        wait(tile_copies(x, xg, i, slot))

        @pl.when(i >= 2)
        def _():
            wait(out_gu(i - 2, slot))

        for k, r in enumerate((dg, du)):
            for n in range(2):
                wgu[slot, k, :, n * 1024 : (n + 1) * 1024] = dot(
                    tile[slot], r[:, n * 1024 : (n + 1) * 1024], 0, 0
                ).astype(BF)
        start(out_gu(i, slot))
        return 0

    lax.fori_loop(0, D // ND, gu_tile, 0)

    def last(k, _):
        pair_send(0, k).wait_recv()

        @pl.when(is_mid)
        def _():
            run_recv(z, k).wait_recv()
            run_recv(4, k).wait_recv()
            add_terms(0, k, (z, 4), dx.at[:, half(k)])

        @pl.when(is_end)
        def _():
            t = jnp.where(z == 0, 4, 3)
            run_recv(t, k).wait_recv()
            add_terms(0, k, (t,), dx.at[:, half(k)])

        return 0

    lax.fori_loop(0, 2, last, 0)
    for i in (D // ND - 2, D // ND - 1):
        wait(out_gu(i, i % 2))
    wait_sends(Dy)
    wait_sends(X)

    def sums(t, _):
        p, k = t // 2, lax.rem(t, 2)
        pair_send(p, k).wait_send()

        @pl.when(p > 0)
        def _():
            run_send(p, k, other, 0).wait_send()

        return 0

    lax.fori_loop(0, 8, sums, 0)


def fused(x, dy, gate, up, w_gate, w_up, w_down):
    hbm = pl.BlockSpec(memory_space=pl.ANY)

    def arr(*shape, dtype=BF):
        return jax.ShapeDtypeStruct(shape, dtype)

    outs = [
        arr(R, D), arr(D, F), arr(D, F), arr(F, D), arr(8, R, D), arr(8, R, D),
        arr(4, R, D, dtype=F32), arr(4, R, D), arr(4, R, D), arr(4, R, D), arr(5, R, D),
    ]
    dma = pltpu.SemaphoreType.DMA
    scratch = [
        pltpu.VMEM((8 * R, F), BF), pltpu.VMEM((8 * R, F), BF), pltpu.VMEM((8 * R, F), BF),
        pltpu.VMEM((2 * R, D), BF), pltpu.VMEM((2, 2 * R, F), BF), pltpu.VMEM((2, NH, D), BF),
        pltpu.VMEM((2, 2, ND, F), BF), pltpu.VMEM((2, 8 * R, ND), BF), pltpu.VMEM((2, F, ND), BF),
        pltpu.VMEM((2, R, ND), F32), pltpu.VMEM((2, R, ND), BF), pltpu.VMEM((R, K2), F32),
        dma((2,)), dma((2, 2)), dma((2, 2)), dma((2,)), dma((2, 8)), dma((2, 2)), dma((2, 2)), dma((5,)),
        dma((4, H)), dma((4, H)), dma((2, 4, H)), dma((8, H)),
        dma((4, Q)), dma((4, Q)), dma((2, 4, Q)), dma((8, Q)),
        dma((4, 2)), dma((4, 2)), dma((4, 2)), dma((5, 2)),
    ]
    return pl.pallas_call(
        kernel,
        out_shape=outs,
        in_specs=[hbm] * 7,
        out_specs=[hbm] * len(outs),
        scratch_shapes=scratch,
        compiler_params=pltpu.CompilerParams(
            collective_id=0, has_side_effects=True, vmem_limit_bytes=67043328
        ),
        cost_estimate=pl.CostEstimate(flops=225_000_000_000, bytes_accessed=500_000_000, transcendentals=4_000_000),
    )(x, dy, gate, up, w_gate, w_up, w_down)[:4]


def solution(mesh):
    rows, mine, cols = P(("dp", "tp"), None), P("dp", "tp"), P(None, "tp")
    return jax.shard_map(
        fused,
        mesh=mesh,
        in_specs=(rows, rows, mine, mine, cols, cols, P("tp", None)),
        out_specs=(rows, mine, mine, rows),
        check_vma=False,
    )
```

time: 800 us -> 419 us (0.52)
  matrix products: 381 us -> 0 us
  Pallas kernels: 0 us -> 369 us
  waiting for transfers between devices: 281 us -> 0 us
  other arithmetic: 36.9 us -> 0.01 us
  local copies, waits for them, and re-layouts: 63.9 us -> 45.2 us
  between operations: 14.3 us -> 0.65 us
  starting transfers between devices: 8.07 us -> 0 us
    dot_general x9 -> x0, matrix products: 381 us -> none  [the longest x6 218 us: by_group(): jnp.einsum('gta,gtb->gab', a, b, preferred_element_type=jnp.float32)]
    pallas_call x0 -> x1, Pallas kernels: none -> 369 us  [fused(): pl.pallas_call(kernel, out_shape=outs, in_specs=[hbm] * 7, out_specs=[hbm...]
    unnamed x5 -> x0, waiting for transfers between devices: 167 us -> none
    dot_general x9 -> x0, waiting for transfers between devices: 115 us -> none  [by_group(): jnp.einsum('gta,gtb->gab', a, b, preferred_element_type=jnp.float32)]
    reshape x2 -> x0, other arithmetic: 36.9 us -> none  [the longest x1 21.8 us: by_group(): return product.astype(jnp.bfloat16).reshape(-1, b.shape[-1])]
    unnamed x7 -> x16, local copies, waits for them, and re-layouts: 62.7 us -> 45.2 us
  transfers between devices with their start and end apart: 12 -> 0, of which waited for: 6 -> 0; matrix products, arithmetic and copies ran while one was open for 60% -> 0% of each run, Pallas kernels for 0% -> 0%
where the time goes in v1:
time: 419 us; the launch traced here: 415 us
  Pallas kernels  369 us (88%)
  local copies, waits for them, and re-layouts  45.2 us (11%)
    pallas_call x1, Pallas kernels, fused(): pl.pallas_call(kernel, out_shape=outs, in_specs=[hbm] * 7, out_specs=[hbm...  369 us
    unnamed x16, local copies, waits for them, and re-layouts  45.2 us

profile of v1, /device:TPU:1, one launch (start us, length us, event | category | flops | bytes accessed | tf_op | source)
XLA Modules:
  0.0 414.9 jit_solution(7518172009608954275)
XLA Ops:
  0.6 369.0 %shard_map.102 = (bf16[224,5120]{1,0:T(8,128)(2,1)}, bf16[5120,2048]{1,0:T(8,128)(2,1)}, bf16[5120,2048]{1,0:T(8,128)(2,1)}, bf16[2048,5120]{1,0:T(8,128)(2,1)},...) custom-call(bf16[224,5120]{1,0:T(8,128)(2,1)} %x.1, ...), custom_call_target="tpu_custom_call" | custom-call | flops 224999997440 | bytes 500000000 | tf_op jit(solution)/shard_map/pallas_call | solution.py:574
  369.7 3.2 copy.15
  372.8 0.0 copy-start
  372.8 0.0 slice-start
  372.8 0.0 slice-start.1
  372.8 0.0 slice-start.2
  372.9 21.2 %copy.16 = bf16[5120,2048]{1,0:T(8,128)(2,1)} copy(bf16[5120,2048]{1,0:T(8,128)(2,1)} %get-tuple-element.17) | data formatting | bytes 41943040
  394.1 0.0 copy-done
  394.1 0.0 slice-start.3
  394.1 0.0 slice-start.4
  394.1 10.6 %copy.17 = bf16[5120,2048]{1,0:T(8,128)(2,1)} copy(bf16[5120,2048]{1,0:T(8,128)(2,1)S(1)} %copy-done) | data formatting | bytes 41943040
  404.7 0.0 slice-done
  404.7 0.0 slice-done.1
  404.7 0.0 slice-done.2
  404.7 1.4 slice-done.3
  406.1 1.2 slice-done.4
  407.3 7.5 %copy.18 = bf16[2048,5120]{1,0:T(8,128)(2,1)} copy(bf16[2048,5120]{1,0:T(8,128)(2,1)S(1)} %bitcast.1) | data formatting | bytes 41943040
  (1 shorter events, 0.0 us)
Async XLA Ops:
  372.8 21.3 %copy-start = (bf16[5120,2048]{1,0:T(8,128)(2,1)S(1)}, bf16[5120,2048]{1,0:T(8,128)(2,1)}, u32[]{:S(2)}) copy-start(bf16[5120,2048]{1,0:T(8,128)(2,1)} %get-tuple-element.18) | copy-start | bytes 62914564
  372.8 31.9 %slice-start = ((s8[20971520]{0:T(1024)(128)(4,1)}), s8[4194304]{0:T(1024)(128)(4,1)S(1)}, s32[]{:S(2)}) async-start(s8[20971520]{0:T(1024)(128)(4,1)} %bitcast), calls=%async_computation | async-start | bytes 8388608
  372.8 31.9 %slice-start.1 = ((s8[20971520]{0:T(1024)(128)(4,1)}), s8[4194304]{0:T(1024)(128)(4,1)S(1)}, s32[]{:S(2)}) async-start(s8[20971520]{0:T(1024)(128)(4,1)} %bitcast), calls=%async_computation.1 | async-start | bytes 8388608
  372.8 31.9 %slice-start.2 = ((s8[20971520]{0:T(1024)(128)(4,1)}), s8[4194304]{0:T(1024)(128)(4,1)S(1)}, s32[]{:S(2)}) async-start(s8[20971520]{0:T(1024)(128)(4,1)} %bitcast), calls=%async_computation.2 | async-start | bytes 8388608
  394.1 12.0 %slice-start.3 = ((s8[20971520]{0:T(1024)(128)(4,1)}), s8[4194304]{0:T(1024)(128)(4,1)S(1)}, s32[]{:S(2)}) async-start(s8[20971520]{0:T(1024)(128)(4,1)} %bitcast), calls=%async_computation.3 | async-start | bytes 8388608
  394.1 13.2 %slice-start.4 = ((s8[20971520]{0:T(1024)(128)(4,1)}), s8[4194304]{0:T(1024)(128)(4,1)S(1)}, s32[]{:S(2)}) async-start(s8[20971520]{0:T(1024)(128)(4,1)} %bitcast), calls=%async_computation.4 | async-start | bytes 8388608

commit v2 on v1

--- a/solution.py
+++ b/solution.py
@@ -19,17 +19,36 @@
 NH = 256
 ND = 512
 K2 = D // 2
+NT = D // ND
+NF = 4
 
 
 def dot(a, b, ca, cb):
     return lax.dot_general(a, b, (((ca,), (cb,)), ((), ())), preferred_element_type=F32)
 
 
+def order(z, p):
+    zz = jnp.where(z < 2, z, 3 - z)
+    near = jnp.where((zz == 1) & (p < 2), 1 - p, p)
+    return jnp.where(z < 2, near, 3 - near)
+
+
+def rows_copies(own, all_, i, dst, sems, block_of, c):
+    cols = pl.ds(i * ND, ND)
+    out = []
+    for p in range(4):
+        b = block_of(p)
+        for k, core in enumerate((c, 1 - c)):
+            src = own.at[:, cols] if p == 0 and k == 0 else all_.at[2 * b + core, :, cols]
+            out.append(pltpu.make_async_copy(src, dst.at[pl.ds((2 * p + k) * R, R)], sems.at[2 * p + k]))
+    return out
+
+
 def kernel(
     x, dy, gate, up, w_gate, w_up, w_down,
-    dx, dwg, dwu, dwd, dyg, xg, pown, psend, precv, rsend, rrecv,
-    hid, dg, du, dyb, gub, wd, wgu, tile, ost, stf, stb, rsf,
-    s_wd, s_wgu, s_gub, s_dyb, s_tile, s_out, s_st, s_rs,
+    dxa, dwg, dwu, dwd, dgo, duo, xg, s_end, s_mid, dyg, pown, psend, precv, rsend, rrecv,
+    hid, dg, du, dyb, gub, wd, wgu, tile, ost, stf, stb, rsf, rsb,
+    s_wd, s_wgu, s_gub, s_dyb, s_tile, s_out, s_st, s_rs, s_keep,
     sd_r, sd_l, sd_p, rd, sx_r, sx_l, sx_p, rx, sp, rp, sr, rr,
 ):
     me = lax.axis_index("tp")
@@ -39,11 +58,9 @@
     right, left = me + 2, me - 2
     is_end = (z == 0) | (z == 3)
     is_mid = (z == 1) | (z == 2)
-    zz = jnp.where(z < 2, z, 3 - z)
 
     def block_of(p):
-        near = jnp.where((zz == 1) & (p < 2), 1 - p, p)
-        return jnp.where(z < 2, near, 3 - near)
+        return order(z, p)
 
     def remote(src, dst, ssem, rsem, to):
         return pltpu.make_async_remote_copy(
@@ -180,16 +197,14 @@
         return pltpu.make_async_copy(src, dyb.at[pl.ds(i * R, R)], s_dyb.at[i])
 
     def tile_copies(own, all_, i, slot):
-        cols = pl.ds(i * ND, ND)
-        out = []
-        for p in range(4):
-            b = block_of(p)
-            for k, core in enumerate((c, 1 - c)):
-                src = own.at[:, cols] if p == 0 and k == 0 else all_.at[2 * b + core, :, cols]
-                out.append(
-                    pltpu.make_async_copy(src, tile.at[slot, pl.ds((2 * p + k) * R, R)], s_tile.at[slot, 2 * p + k])
-                )
-        return out
+        return rows_copies(own, all_, i, tile.at[slot], s_tile.at[slot], block_of, c)
+
+    def keep(p):
+        rows = pl.ds(pl.multiple_of(p * 2 * R, 2 * R), 2 * R)
+        return [
+            pltpu.make_async_copy(src.at[rows], dst.at[rows], s_keep.at[k, p])
+            for k, (src, dst) in enumerate(((dg, dgo), (du, duo)))
+        ]
 
     def start(copies):
         for cp in copies:
@@ -214,39 +229,40 @@
     def add_terms(p, k, extra, out):
         loads = [
             pltpu.make_async_copy(pown.at[p, :, half(k)], rsf, s_rs.at[0]),
-            pltpu.make_async_copy(precv.at[p, :, half(k)], dyb.at[pl.ds(0, R), pl.ds(0, K2)], s_rs.at[1]),
+            pltpu.make_async_copy(precv.at[p, :, half(k)], rsb.at[0], s_rs.at[1]),
         ]
-        for n, t in enumerate(extra):
-            loads.append(
-                pltpu.make_async_copy(
-                    rrecv.at[t, :, half(k)], dyb.at[pl.ds(R, R), pl.ds(n * K2, K2)], s_rs.at[2 + n]
-                )
-            )
+        for t in extra:
+            loads.append(pltpu.make_async_copy(rrecv.at[t, :, half(k)], rsb.at[1], s_rs.at[2]))
         start(loads)
         wait(loads)
+        wide = out.dtype == F32
 
         def body(i, _):
             rows = pl.ds(pl.multiple_of(i * 32, 32), 32)
-            low = pl.ds(pl.multiple_of(R + i * 32, 32), 32)
-            v = rsf[rows] + dyb[rows, 0:K2].astype(F32)
-            for n in range(len(extra)):
-                v = v + dyb[low, n * K2 : (n + 1) * K2].astype(F32)
-            dyb[rows, K2:D] = v.astype(BF)
+            v = rsf[rows] + rsb[0, rows].astype(F32)
+            if extra:
+                v = v + rsb[1, rows].astype(F32)
+            if wide:
+                rsf[rows] = v
+            else:
+                rsb[2, rows] = v.astype(BF)
             return 0
 
         lax.fori_loop(0, R // 32, body, 0)
-        cp = pltpu.make_async_copy(dyb.at[pl.ds(0, R), pl.ds(K2, K2)], out, s_rs.at[4])
+        cp = pltpu.make_async_copy(rsf if wide else rsb.at[2], out, s_rs.at[3])
         cp.start()
         cp.wait()
 
-    def pass_on(p, k, mid):
+    def sum_up(p, k, mid, out):
         t = block_of(p)
         pair_send(p, k).wait_recv()
-        extra = ()
         if mid:
             run_recv(t, k).wait_recv()
-            extra = (t,)
-        add_terms(p, k, extra, rsend.at[p, :, half(k)])
+        add_terms(p, k, (t,) if mid else (), out)
+        return t
+
+    def pass_on(p, k, mid):
+        t = sum_up(p, k, mid, rsend.at[p, :, half(k)])
 
         @pl.when(t > z)
         def _():
@@ -256,9 +272,9 @@
         def _():
             run_send(p, k, left, jnp.where(t == z - 1, 4, t)).start()
 
-    def pass_on_both(p, mid):
+    def halves(f):
         def body(k, _):
-            pass_on(p, k, mid)
+            f(k)
             return 0
 
         lax.fori_loop(0, 2, body, 0)
@@ -357,6 +373,8 @@
 
         lax.fori_loop(0, F // NH, hidden_tile, 0)
 
+        start(keep(p))
+
         @pl.when(p < 3)
         def _():
             start(gub_copies(p + 1))
@@ -368,10 +386,6 @@
         @pl.when(p >= 2)
         def _():
             x_step(2 * p - 3)
-
-            @pl.when(is_end)
-            def _():
-                pass_on_both(p - 1, False)
 
         def stage(j, slot):
             cols = pl.ds(pl.multiple_of(j * ND, ND), ND)
@@ -418,6 +432,10 @@
         def _():
             x_step(2 * p - 2)
 
+            @pl.when(is_end)
+            def _():
+                halves(lambda k: pass_on(p, k, False))
+
         return 0
 
     lax.fori_loop(0, 4, phase, 0)
@@ -434,10 +452,6 @@
         @pl.when(i < D // ND - 1)
         def _():
             start(tile_copies(dy, dyg, i + 1, 1 - slot))
-
-        @pl.when((i == 0) & is_end)
-        def _():
-            pass_on_both(3, False)
 
         @pl.when((i == 2) | (i == 4))
         def _():
@@ -474,29 +488,21 @@
         slot = lax.rem(i, 2)
         q = i // 2
 
-        @pl.when((slot == 0) & (q < Q - 1))
+        @pl.when((slot == 0) & (q < NF // 2 - 1))
         def _():
             x_end(q + 1)
 
-        @pl.when((slot == 1) & (q < Q - 1))
+        @pl.when((slot == 1) & (q < NF // 2 - 1))
         def _():
             x_ready(q + 1)
 
-        @pl.when(i < D // ND - 1)
+        @pl.when(i < NF - 1)
         def _():
             start(tile_copies(x, xg, i + 1, 1 - slot))
 
-        @pl.when(is_mid & ((i == 2) | (i == 4)))
-        def _():
-            pass_on(3, i // 2 - 1, True)
-
-        @pl.when(is_mid & (i == 5))
-        def _():
-            pass_on_both(2, True)
-
-        @pl.when(is_mid & ((i == 6) | (i == 8)))
-        def _():
-            pass_on(1, i // 2 - 3, True)
+        @pl.when(is_mid & ((i == 0) | (i == 2)))
+        def _():
+            pass_on(3, i // 2, True)
 
         wait(tile_copies(x, xg, i, slot))
 
@@ -512,27 +518,35 @@
         start(out_gu(i, slot))
         return 0
 
-    lax.fori_loop(0, D // ND, gu_tile, 0)
-
-    def last(k, _):
+    lax.fori_loop(0, NF, gu_tile, 0)
+
+    for i in range(NF // 2, Q):
+        x_end(i)
+
+    @pl.when(is_mid)
+    def _():
+        halves(lambda k: sum_up(1, k, True, s_end.at[:, half(k)]))
+        halves(lambda k: sum_up(2, k, True, s_mid.at[:, half(k)]))
+
+    def own_rows(k):
         pair_send(0, k).wait_recv()
 
         @pl.when(is_mid)
         def _():
-            run_recv(z, k).wait_recv()
-            run_recv(4, k).wait_recv()
-            add_terms(0, k, (z, 4), dx.at[:, half(k)])
+            t = jnp.where(z == 1, 1, 4)
+            run_recv(t, k).wait_recv()
+            add_terms(0, k, (t,), dxa.at[:, half(k)])
 
         @pl.when(is_end)
         def _():
-            t = jnp.where(z == 0, 4, 3)
-            run_recv(t, k).wait_recv()
-            add_terms(0, k, (t,), dx.at[:, half(k)])
-
-        return 0
-
-    lax.fori_loop(0, 2, last, 0)
-    for i in (D // ND - 2, D // ND - 1):
+            add_terms(0, k, (), dxa.at[:, half(k)])
+
+    halves(own_rows)
+    for i in range(NF // 2, Q):
+        x_ready(i)
+    for p in range(4):
+        wait(keep(p))
+    for i in (NF - 2, NF - 1):
         wait(out_gu(i, i % 2))
     wait_sends(Dy)
     wait_sends(X)
@@ -541,13 +555,141 @@
         p, k = t // 2, lax.rem(t, 2)
         pair_send(p, k).wait_send()
 
-        @pl.when(p > 0)
+        @pl.when((is_end & (p > 0)) | (is_mid & (p == 3)))
         def _():
             run_send(p, k, other, 0).wait_send()
 
         return 0
 
     lax.fori_loop(0, 8, sums, 0)
+
+
+def rest(
+    x, xg, dgi, dui, dwg_in, dwu_in, dwd_in, dwg, dwu, dwd,
+    dg, du, tile, ost, bg, bd, s_in, s_tile, s_out, s_ci, s_co,
+):
+    me = lax.axis_index("tp")
+    z = me // 2
+    c = lax.rem(me, 2)
+
+    def tile_copies(i, slot):
+        return rows_copies(x, xg, i, tile.at[slot], s_tile.at[slot], lambda p: order(z, p), c)
+
+    def moves(i, slot, out):
+        rows = pl.ds(pl.multiple_of(i * ND, ND), ND)
+        copies = []
+        for k, (src, dst, buf) in enumerate(
+            ((dwg_in, dwg, bg.at[slot, 0]), (dwu_in, dwu, bg.at[slot, 1]), (dwd_in, dwd, bd.at[slot]))
+        ):
+            if out:
+                copies.append(pltpu.make_async_copy(buf, dst.at[rows], s_co.at[slot, k]))
+            else:
+                copies.append(pltpu.make_async_copy(src.at[rows], buf, s_ci.at[slot, k]))
+        return copies
+
+    def out_gu(i, slot):
+        rows = pl.ds(pl.multiple_of(i * ND, ND), ND)
+        return [
+            pltpu.make_async_copy(ost.at[slot, k], (dwg, dwu)[k].at[rows], s_out.at[slot, k]) for k in range(2)
+        ]
+
+    def start(copies):
+        for cp in copies:
+            cp.start()
+
+    def wait(copies):
+        for cp in copies:
+            cp.wait()
+
+    whole = [pltpu.make_async_copy(s, d, s_in.at[k]) for k, (s, d) in enumerate(((dgi, dg), (dui, du)))]
+    start(tile_copies(NF, 0))
+    start(whole)
+
+    def step(i, _):
+        slot = lax.rem(i, 2)
+
+        @pl.when(i < NT - NF - 1)
+        def _():
+            start(tile_copies(NF + i + 1, 1 - slot))
+
+        wait(tile_copies(NF + i, slot))
+
+        @pl.when(i >= 2)
+        def _():
+            wait(out_gu(NF + i - 2, slot))
+
+        @pl.when((i >= 1) & (i < NF + 1))
+        def _():
+            wait(moves(i - 1, 1 - slot, False))
+            start(moves(i - 1, 1 - slot, True))
+
+        @pl.when((i >= 2) & (i < NF + 2))
+        def _():
+            wait(moves(i - 2, slot, True))
+
+        @pl.when((i >= 2) & (i < NF))
+        def _():
+            start(moves(i, slot, False))
+
+        for k, r in enumerate((dg, du)):
+
+            @pl.when(i == 0)
+            def _():
+                whole[k].wait()
+                if k:
+                    start(moves(0, 0, False))
+                    start(moves(1, 1, False))
+
+            for n in range(2):
+                ost[slot, k, :, n * 1024 : (n + 1) * 1024] = dot(
+                    tile[slot], r[:, n * 1024 : (n + 1) * 1024], 0, 0
+                ).astype(BF)
+        start(out_gu(NF + i, slot))
+        return 0
+
+    lax.fori_loop(0, NT - NF, step, 0)
+    for i in (NT - NF - 2, NT - NF - 1):
+        wait(out_gu(NF + i, i % 2))
+
+
+def finish(dxa, from_mid, across, dx, own, got, out, s_own, s_got, s_out):
+    z = lax.axis_index("tp") // 2
+    is_end = (z == 0) | (z == 3)
+    n = R // 32
+
+    def at(i):
+        return pl.ds(pl.multiple_of(i * 32, 32), 32)
+
+    def get(src, dst, sem, i):
+        return pltpu.make_async_copy(src.at[at(i)], dst.at[at(i)], sem.at[i])
+
+    def load(i, _):
+        get(dxa, own, s_own, i).start()
+
+        @pl.when(is_end)
+        def _():
+            get(from_mid, got, s_got, i).start()
+
+        @pl.when(jnp.logical_not(is_end))
+        def _():
+            get(across, got, s_got, i).start()
+
+        return 0
+
+    def add(i, _):
+        get(dxa, own, s_own, i).wait()
+        get(from_mid, got, s_got, i).wait()
+        out[at(i)] = (own[at(i)] + got[at(i)].astype(F32)).astype(BF)
+        get(out, dx, s_out, i).start()
+        return 0
+
+    def end(i, _):
+        get(out, dx, s_out, i).wait()
+        return 0
+
+    lax.fori_loop(0, n, load, 0)
+    lax.fori_loop(0, n, add, 0)
+    lax.fori_loop(0, n, end, 0)
 
 
 def fused(x, dy, gate, up, w_gate, w_up, w_down):
@@ -556,9 +698,10 @@
     def arr(*shape, dtype=BF):
         return jax.ShapeDtypeStruct(shape, dtype)
 
+    part = arr(NF * ND, F)
     outs = [
-        arr(R, D), arr(D, F), arr(D, F), arr(F, D), arr(8, R, D), arr(8, R, D),
-        arr(4, R, D, dtype=F32), arr(4, R, D), arr(4, R, D), arr(4, R, D), arr(5, R, D),
+        arr(R, D, dtype=F32), part, part, arr(F, D), arr(8 * R, F), arr(8 * R, F), arr(8, R, D), arr(R, D), arr(R, D),
+        arr(8, R, D), arr(4, R, D, dtype=F32), arr(4, R, D), arr(4, R, D), arr(4, R, D), arr(5, R, D),
     ]
     dma = pltpu.SemaphoreType.DMA
     scratch = [
@@ -566,22 +709,51 @@
         pltpu.VMEM((2 * R, D), BF), pltpu.VMEM((2, 2 * R, F), BF), pltpu.VMEM((2, NH, D), BF),
         pltpu.VMEM((2, 2, ND, F), BF), pltpu.VMEM((2, 8 * R, ND), BF), pltpu.VMEM((2, F, ND), BF),
         pltpu.VMEM((2, R, ND), F32), pltpu.VMEM((2, R, ND), BF), pltpu.VMEM((R, K2), F32),
-        dma((2,)), dma((2, 2)), dma((2, 2)), dma((2,)), dma((2, 8)), dma((2, 2)), dma((2, 2)), dma((5,)),
+        pltpu.VMEM((3, R, K2), BF),
+        dma((2,)), dma((2, 2)), dma((2, 2)), dma((2,)), dma((2, 8)), dma((2, 2)), dma((2, 2)), dma((4,)), dma((2, 4)),
         dma((4, H)), dma((4, H)), dma((2, 4, H)), dma((8, H)),
         dma((4, Q)), dma((4, Q)), dma((2, 4, Q)), dma((8, Q)),
         dma((4, 2)), dma((4, 2)), dma((4, 2)), dma((5, 2)),
     ]
-    return pl.pallas_call(
+    made = pl.pallas_call(
         kernel,
         out_shape=outs,
         in_specs=[hbm] * 7,
         out_specs=[hbm] * len(outs),
         scratch_shapes=scratch,
-        compiler_params=pltpu.CompilerParams(
-            collective_id=0, has_side_effects=True, vmem_limit_bytes=67043328
-        ),
-        cost_estimate=pl.CostEstimate(flops=225_000_000_000, bytes_accessed=500_000_000, transcendentals=4_000_000),
-    )(x, dy, gate, up, w_gate, w_up, w_down)[:4]
+        compiler_params=pltpu.CompilerParams(collective_id=0, has_side_effects=True, vmem_limit_bytes=67043328),
+        cost_estimate=pl.CostEstimate(flops=180_000_000_000, bytes_accessed=500_000_000, transcendentals=4_000_000),
+    )(x, dy, gate, up, w_gate, w_up, w_down)
+    dxa, dwg, dwu, dwd, dgo, duo, xg, s_end, s_mid = made[:9]
+    cores = range(2)
+    from_mid = lax.ppermute(s_end, "tp", [(2 * a + k, 2 * b + k) for a, b in ((1, 0), (2, 3)) for k in cores])
+    across = lax.ppermute(s_mid, "tp", [(2 * a + k, 2 * b + k) for a, b in ((1, 2), (2, 1)) for k in cores])
+    full = [arr(D, F), arr(D, F), arr(F, D)]
+    dwg, dwu, dwd = pl.pallas_call(
+        rest,
+        out_shape=full,
+        in_specs=[hbm] * 7,
+        out_specs=[hbm] * 3,
+        scratch_shapes=[
+            pltpu.VMEM((8 * R, F), BF), pltpu.VMEM((8 * R, F), BF), pltpu.VMEM((2, 8 * R, ND), BF),
+            pltpu.VMEM((2, 2, ND, F), BF), pltpu.VMEM((2, 2, ND, F), BF), pltpu.VMEM((2, ND, D), BF),
+            dma((2,)), dma((2, 8)), dma((2, 2)), dma((2, 3)), dma((2, 3)),
+        ],
+        compiler_params=pltpu.CompilerParams(vmem_limit_bytes=67043328),
+        cost_estimate=pl.CostEstimate(flops=45_000_000_000, bytes_accessed=150_000_000, transcendentals=0),
+    )(x, xg, dgo, duo, dwg, dwu, dwd)
+    dx = pl.pallas_call(
+        finish,
+        out_shape=arr(R, D),
+        in_specs=[hbm] * 3,
+        out_specs=hbm,
+        scratch_shapes=[
+            pltpu.VMEM((R, D), F32), pltpu.VMEM((R, D), BF), pltpu.VMEM((R, D), BF), dma((7,)), dma((7,)), dma((7,)),
+        ],
+        compiler_params=pltpu.CompilerParams(vmem_limit_bytes=67043328),
+        cost_estimate=pl.CostEstimate(flops=3_000_000, bytes_accessed=12_000_000, transcendentals=0),
+    )(dxa, from_mid, across)
+    return dx, dwg, dwu, dwd
 
 
 def solution(mesh):

time: 419 us -> 385 us (0.919)
  local copies, waits for them, and re-layouts: 45.2 us -> 0 us
  Pallas kernels: 369 us -> 374 us
    pallas_call x0 -> x2, Pallas kernels: none -> 65.5 us  [the longest x1 61.1 us: fused(): pl.pallas_call(rest, out_shape=full, in_specs=[hbm] * 7, out_specs=[hbm]...]
    pallas_call x1, Pallas kernels: 369 us -> 309 us  [fused(): pl.pallas_call(kernel, out_shape=outs, in_specs=[hbm] * 7, out_specs=[hbm...]
    unnamed x16 -> x0, local copies, waits for them, and re-layouts: 45.2 us -> none
  transfers between devices with their start and end apart: 0 -> 2, of which waited for: 0 -> 0; matrix products, arithmetic and copies ran while one was open for 0% -> 0% of each run, Pallas kernels for 0% -> 16%
where the time goes in v2:
time: 385 us; the launch traced here: 378 us
  Pallas kernels  374 us (97%)
    pallas_call x1, Pallas kernels, fused(): pl.pallas_call(kernel, out_shape=outs, in_specs=[hbm] * 7, out_specs=[hbm...  309 us
    pallas_call x1, Pallas kernels, fused(): pl.pallas_call(rest, out_shape=full, in_specs=[hbm] * 7, out_specs=[hbm]...  61.1 us
  transfers between devices with their start and end apart: 2, of which 0 were waited for; matrix products, arithmetic and copies ran while one was open for 0% of the time, Pallas kernels for 16%

profile of v2, /device:TPU:1, one launch (start us, length us, event | category | flops | bytes accessed | tf_op | source)
XLA Modules:
  0.0 378.5 jit_solution(1291082329575317807)
XLA Ops:
  0.6 308.8 %shard_map.102 = (f32[224,5120]{1,0:T(8,128)}, bf16[2048,2048]{1,0:T(8,128)(2,1)}, bf16[2048,2048]{1,0:T(8,128)(2,1)}, bf16[2048,5120]{1,0:T(8,128)(2,1)}, bf16[...) custom-call(bf16[224,5120]{1,0:T(8,128)(2,1)} %x.3, ...), custom_call_target="tpu_custom_call" | custom-call | flops 179999997952 | bytes 500000000 | tf_op jit(solution)/shard_map/pallas_call | solution.py:718
  309.4 1.3 collective-permute-start
  310.7 2.1 collective-permute-start.1
  312.8 61.1 %shard_map.104 = (bf16[5120,2048]{1,0:T(8,128)(2,1)}, bf16[5120,2048]{1,0:T(8,128)(2,1)}, bf16[2048,5120]{1,0:T(8,128)(2,1)}) custom-call(bf16[224,5120]{1,0:T(8,128)(2,1)} %x.3, bf16[8,224,5120]{2,1,0:T(8,128)(2,1)} %get-tuple-element.19.xg, bf16[1792,2048]{1,0:T(8,128)(2,1)} %get-tuple-element.20.dgi, bf16[1792,2048]{1,0:T(8,128)(2,1)} %get-tuple-element.21.dui, ...), custom_call_target="tpu_custom_call" | custom-call | flops 44999999488 | bytes 150000000 | tf_op jit(solution)/shard_map/pallas_call | solution.py:732
  373.9 0.0 collective-permute-done.from_mid
  373.9 0.0 collective-permute-done.1.across
  373.9 4.4 %shard_map.103 = bf16[224,5120]{1,0:T(8,128)(2,1)} custom-call(f32[224,5120]{1,0:T(8,128)} %get-tuple-element.16.dxa, bf16[224,5120]{1,0:T(8,128)(2,1)} %collective-permute-done.from_mid, bf16[224,5120]{1,0:T(8,128)(2,1)} %collective-permute-done.1.across), custom_call_target="tpu_custom_call" | custom-call | flops 3000000 | bytes 12000000 | tf_op jit(solution)/shard_map/pallas_call | solution.py:745
Async XLA Ops:
  309.4 64.5 %collective-permute-start = (bf16[224,5120]{1,0:T(8,128)(2,1)}, bf16[224,5120]{1,0:T(8,128)(2,1)}, u32[]{:S(2)}, u32[]{:S(2)}) collective-permute-start(bf16[224,5120]{1,0:T(8,128)(2,1)} %get-tuple-element.17), channel_id=1, source_target_pairs={{2,0},{3,1},{4,6},{5,7},{10,8},{11,9},{12,14},{13,15},{18,16},{19,... | collective-permute-start | bytes 6881288 | tf_op jit(solution)/shard_map/ppermute | solution.py:729
  310.7 63.2 %collective-permute-start.1 = (bf16[224,5120]{1,0:T(8,128)(2,1)}, bf16[224,5120]{1,0:T(8,128)(2,1)}, u32[]{:S(2)}, u32[]{:S(2)}) collective-permute-start(bf16[224,5120]{1,0:T(8,128)(2,1)} %get-tuple-element.18), channel_id=1, source_target_pairs={{2,4},{3,5},{4,2},{5,3},{10,12},{11,13},{12,10},{13,11},{18,20},{1... | collective-permute-start | bytes 6881288 | tf_op jit(solution)/shard_map/ppermute | solution.py:730

commit v3 on v2

--- a/solution.py
+++ b/solution.py
@@ -19,8 +19,11 @@
 NH = 256
 ND = 512
 K2 = D // 2
+RC = 32
 NT = D // ND
 NF = 4
+NQ = (NF + 1) // 2
+NM = 4
 
 
 def dot(a, b, ca, cb):
@@ -227,18 +230,29 @@
         return remote(rsend.at[p, :, half(k)], rrecv.at[t, :, half(k)], sr.at[p, k], rr.at[t, k], to)
 
     def add_terms(p, k, extra, out):
-        loads = [
-            pltpu.make_async_copy(pown.at[p, :, half(k)], rsf, s_rs.at[0]),
-            pltpu.make_async_copy(precv.at[p, :, half(k)], rsb.at[0], s_rs.at[1]),
-        ]
-        for t in extra:
-            loads.append(pltpu.make_async_copy(rrecv.at[t, :, half(k)], rsb.at[1], s_rs.at[2]))
-        start(loads)
-        wait(loads)
         wide = out.dtype == F32
+        srcs = [(pown.at[p], rsf), (precv.at[p], rsb.at[0])] + [(rrecv.at[t], rsb.at[1]) for t in extra]
+        res = rsf if wide else rsb.at[2]
+
+        def at(i):
+            return pl.ds(pl.multiple_of(i * RC, RC), RC)
+
+        def loads(i):
+            return [
+                pltpu.make_async_copy(src.at[at(i), half(k)], dst.at[at(i)], s_rs.at[n, i])
+                for n, (src, dst) in enumerate(srcs)
+            ]
+
+        def store(i):
+            return pltpu.make_async_copy(res.at[at(i)], out.at[at(i), half(k)], s_rs.at[3, i])
+
+        def first(i, _):
+            start(loads(i))
+            return 0
 
         def body(i, _):
-            rows = pl.ds(pl.multiple_of(i * 32, 32), 32)
+            wait(loads(i))
+            rows = at(i)
             v = rsf[rows] + rsb[0, rows].astype(F32)
             if extra:
                 v = v + rsb[1, rows].astype(F32)
@@ -246,12 +260,15 @@
                 rsf[rows] = v
             else:
                 rsb[2, rows] = v.astype(BF)
+            store(i).start()
             return 0
 
-        lax.fori_loop(0, R // 32, body, 0)
-        cp = pltpu.make_async_copy(rsf if wide else rsb.at[2], out, s_rs.at[3])
-        cp.start()
-        cp.wait()
+        def final(i, _):
+            store(i).wait()
+            return 0
+
+        for f in (first, body, final):
+            lax.fori_loop(0, R // RC, f, 0)
 
     def sum_up(p, k, mid, out):
         t = block_of(p)
@@ -262,7 +279,7 @@
         return t
 
     def pass_on(p, k, mid):
-        t = sum_up(p, k, mid, rsend.at[p, :, half(k)])
+        t = sum_up(p, k, mid, rsend.at[p])
 
         @pl.when(t > z)
         def _():
@@ -488,11 +505,11 @@
         slot = lax.rem(i, 2)
         q = i // 2
 
-        @pl.when((slot == 0) & (q < NF // 2 - 1))
+        @pl.when((slot == 0) & (q < NQ - 1))
         def _():
             x_end(q + 1)
 
-        @pl.when((slot == 1) & (q < NF // 2 - 1))
+        @pl.when((slot == 1) & (q < NQ - 1))
         def _():
             x_ready(q + 1)
 
@@ -500,9 +517,9 @@
         def _():
             start(tile_copies(x, xg, i + 1, 1 - slot))
 
-        @pl.when(is_mid & ((i == 0) | (i == 2)))
-        def _():
-            pass_on(3, i // 2, True)
+        @pl.when(is_mid & ((i == 1) | (i == NF - 1)))
+        def _():
+            pass_on(3, i // (NF - 1), True)
 
         wait(tile_copies(x, xg, i, slot))
 
@@ -520,13 +537,13 @@
 
     lax.fori_loop(0, NF, gu_tile, 0)
 
-    for i in range(NF // 2, Q):
+    for i in range(NQ, Q):
         x_end(i)
 
     @pl.when(is_mid)
     def _():
-        halves(lambda k: sum_up(1, k, True, s_end.at[:, half(k)]))
-        halves(lambda k: sum_up(2, k, True, s_mid.at[:, half(k)]))
+        sum_up(1, 0, True, s_end)
+        halves(lambda k: sum_up(2, k, True, s_mid))
 
     def own_rows(k):
         pair_send(0, k).wait_recv()
@@ -535,14 +552,19 @@
         def _():
             t = jnp.where(z == 1, 1, 4)
             run_recv(t, k).wait_recv()
-            add_terms(0, k, (t,), dxa.at[:, half(k)])
+            add_terms(0, k, (t,), dxa)
 
         @pl.when(is_end)
         def _():
-            add_terms(0, k, (), dxa.at[:, half(k)])
+            add_terms(0, k, (), dxa)
 
     halves(own_rows)
-    for i in range(NF // 2, Q):
+
+    @pl.when(is_mid)
+    def _():
+        sum_up(1, 1, True, s_end)
+
+    for i in range(NQ, Q):
         x_ready(i)
     for p in range(4):
         wait(keep(p))
@@ -576,11 +598,12 @@
         return rows_copies(x, xg, i, tile.at[slot], s_tile.at[slot], lambda p: order(z, p), c)
 
     def moves(i, slot, out):
-        rows = pl.ds(pl.multiple_of(i * ND, ND), ND)
         copies = []
         for k, (src, dst, buf) in enumerate(
             ((dwg_in, dwg, bg.at[slot, 0]), (dwu_in, dwu, bg.at[slot, 1]), (dwd_in, dwd, bd.at[slot]))
         ):
+            n = buf.shape[0]
+            rows = pl.ds(pl.multiple_of(i * n, n), n)
             if out:
                 copies.append(pltpu.make_async_copy(buf, dst.at[rows], s_co.at[slot, k]))
             else:
@@ -601,9 +624,14 @@
         for cp in copies:
             cp.wait()
 
-    whole = [pltpu.make_async_copy(s, d, s_in.at[k]) for k, (s, d) in enumerate(((dgi, dg), (dui, du)))]
+    def whole(k, n):
+        cols = pl.ds(n * 1024, 1024)
+        return pltpu.make_async_copy((dgi, dui)[k].at[:, cols], (dg, du)[k].at[:, cols], s_in.at[k, n])
+
     start(tile_copies(NF, 0))
-    start(whole)
+    for k in range(2):
+        for n in range(2):
+            whole(k, n).start()
 
     def step(i, _):
         slot = lax.rem(i, 2)
@@ -618,29 +646,29 @@
         def _():
             wait(out_gu(NF + i - 2, slot))
 
-        @pl.when((i >= 1) & (i < NF + 1))
+        @pl.when((i >= 1) & (i < NM + 1))
         def _():
             wait(moves(i - 1, 1 - slot, False))
             start(moves(i - 1, 1 - slot, True))
 
-        @pl.when((i >= 2) & (i < NF + 2))
+        @pl.when((i >= 2) & (i < NM + 2))
         def _():
             wait(moves(i - 2, slot, True))
 
-        @pl.when((i >= 2) & (i < NF))
+        @pl.when((i >= 2) & (i < NM))
         def _():
             start(moves(i, slot, False))
 
         for k, r in enumerate((dg, du)):
-
-            @pl.when(i == 0)
-            def _():
-                whole[k].wait()
-                if k:
-                    start(moves(0, 0, False))
-                    start(moves(1, 1, False))
-
             for n in range(2):
+
+                @pl.when(i == 0)
+                def _():
+                    whole(k, n).wait()
+                    if k and n:
+                        start(moves(0, 0, False))
+                        start(moves(1, 1, False))
+
                 ost[slot, k, :, n * 1024 : (n + 1) * 1024] = dot(
                     tile[slot], r[:, n * 1024 : (n + 1) * 1024], 0, 0
                 ).astype(BF)
@@ -648,6 +676,12 @@
         return 0
 
     lax.fori_loop(0, NT - NF, step, 0)
+    if NT - NF == NM:
+        wait(moves(NM - 1, (NM - 1) % 2, False))
+        start(moves(NM - 1, (NM - 1) % 2, True))
+    for i in (NM - 2, NM - 1):
+        if i + 2 > NT - NF - 1:
+            wait(moves(i, i % 2, True))
     for i in (NT - NF - 2, NT - NF - 1):
         wait(out_gu(NF + i, i % 2))
 
@@ -710,7 +744,7 @@
         pltpu.VMEM((2, 2, ND, F), BF), pltpu.VMEM((2, 8 * R, ND), BF), pltpu.VMEM((2, F, ND), BF),
         pltpu.VMEM((2, R, ND), F32), pltpu.VMEM((2, R, ND), BF), pltpu.VMEM((R, K2), F32),
         pltpu.VMEM((3, R, K2), BF),
-        dma((2,)), dma((2, 2)), dma((2, 2)), dma((2,)), dma((2, 8)), dma((2, 2)), dma((2, 2)), dma((4,)), dma((2, 4)),
+        dma((2,)), dma((2, 2)), dma((2, 2)), dma((2,)), dma((2, 8)), dma((2, 2)), dma((2, 2)), dma((4, R // RC)), dma((2, 4)),
         dma((4, H)), dma((4, H)), dma((2, 4, H)), dma((8, H)),
         dma((4, Q)), dma((4, Q)), dma((2, 4, Q)), dma((8, Q)),
         dma((4, 2)), dma((4, 2)), dma((4, 2)), dma((5, 2)),
@@ -736,8 +770,8 @@
         out_specs=[hbm] * 3,
         scratch_shapes=[
             pltpu.VMEM((8 * R, F), BF), pltpu.VMEM((8 * R, F), BF), pltpu.VMEM((2, 8 * R, ND), BF),
-            pltpu.VMEM((2, 2, ND, F), BF), pltpu.VMEM((2, 2, ND, F), BF), pltpu.VMEM((2, ND, D), BF),
-            dma((2,)), dma((2, 8)), dma((2, 2)), dma((2, 3)), dma((2, 3)),
+            pltpu.VMEM((2, 2, ND, F), BF), pltpu.VMEM((2, 2, NF * ND // NM, F), BF), pltpu.VMEM((2, F // NM, D), BF),
+            dma((2, 2)), dma((2, 8)), dma((2, 2)), dma((2, 3)), dma((2, 3)),
         ],
         compiler_params=pltpu.CompilerParams(vmem_limit_bytes=67043328),
         cost_estimate=pl.CostEstimate(flops=45_000_000_000, bytes_accessed=150_000_000, transcendentals=0),

time: 385 us -> 383 us (level)
  no operation moved by 1% of the time
where the time goes in v3:
time: 383 us; the launch traced here: 378 us
  Pallas kernels  374 us (98%)
    pallas_call x1, Pallas kernels, fused(): pl.pallas_call(kernel, out_shape=outs, in_specs=[hbm] * 7, out_specs=[hbm...  307 us
    pallas_call x1, Pallas kernels, fused(): pl.pallas_call(rest, out_shape=full, in_specs=[hbm] * 7, out_specs=[hbm]...  62 us
  transfers between devices with their start and end apart: 2, of which 0 were waited for; matrix products, arithmetic and copies ran while one was open for 0% of the time, Pallas kernels for 16%

profile of v3, /device:TPU:1, one launch (start us, length us, event | category | flops | bytes accessed | tf_op | source)
XLA Modules:
  0.0 377.9 jit_solution(5744142710056920020)
XLA Ops:
  0.6 307.3 %shard_map.102 = (f32[224,5120]{1,0:T(8,128)}, bf16[2048,2048]{1,0:T(8,128)(2,1)}, bf16[2048,2048]{1,0:T(8,128)(2,1)}, bf16[2048,5120]{1,0:T(8,128)(2,1)}, bf16[...) custom-call(bf16[224,5120]{1,0:T(8,128)(2,1)} %x.3, ...), custom_call_target="tpu_custom_call" | custom-call | flops 179999997952 | bytes 500000000 | tf_op jit(solution)/shard_map/pallas_call | solution.py:752
  307.9 1.3 collective-permute-start
  309.2 2.1 collective-permute-start.1
  311.3 62.0 %shard_map.104 = (bf16[5120,2048]{1,0:T(8,128)(2,1)}, bf16[5120,2048]{1,0:T(8,128)(2,1)}, bf16[2048,5120]{1,0:T(8,128)(2,1)}) custom-call(bf16[224,5120]{1,0:T(8,128)(2,1)} %x.3, bf16[8,224,5120]{2,1,0:T(8,128)(2,1)} %get-tuple-element.19.xg, bf16[1792,2048]{1,0:T(8,128)(2,1)} %get-tuple-element.20.dgi, bf16[1792,2048]{1,0:T(8,128)(2,1)} %get-tuple-element.21.dui, ...), custom_call_target="tpu_custom_call" | custom-call | flops 44999999488 | bytes 150000000 | tf_op jit(solution)/shard_map/pallas_call | solution.py:766
  373.3 0.0 collective-permute-done.from_mid
  373.3 0.0 collective-permute-done.1.across
  373.3 4.4 %shard_map.103 = bf16[224,5120]{1,0:T(8,128)(2,1)} custom-call(f32[224,5120]{1,0:T(8,128)} %get-tuple-element.16.dxa, bf16[224,5120]{1,0:T(8,128)(2,1)} %collective-permute-done.from_mid, bf16[224,5120]{1,0:T(8,128)(2,1)} %collective-permute-done.1.across), custom_call_target="tpu_custom_call" | custom-call | flops 3000000 | bytes 12000000 | tf_op jit(solution)/shard_map/pallas_call | solution.py:779
Async XLA Ops:
  307.9 65.4 %collective-permute-start = (bf16[224,5120]{1,0:T(8,128)(2,1)}, bf16[224,5120]{1,0:T(8,128)(2,1)}, u32[]{:S(2)}, u32[]{:S(2)}) collective-permute-start(bf16[224,5120]{1,0:T(8,128)(2,1)} %get-tuple-element.17), channel_id=1, source_target_pairs={{2,0},{3,1},{4,6},{5,7},{10,8},{11,9},{12,14},{13,15},{18,16},{19,... | collective-permute-start | bytes 6881288 | tf_op jit(solution)/shard_map/ppermute | solution.py:763
  309.2 64.1 %collective-permute-start.1 = (bf16[224,5120]{1,0:T(8,128)(2,1)}, bf16[224,5120]{1,0:T(8,128)(2,1)}, u32[]{:S(2)}, u32[]{:S(2)}) collective-permute-start(bf16[224,5120]{1,0:T(8,128)(2,1)} %get-tuple-element.18), channel_id=1, source_target_pairs={{2,4},{3,5},{4,2},{5,3},{10,12},{11,13},{12,10},{13,11},{18,20},{1... | collective-permute-start | bytes 6881288 | tf_op jit(solution)/shard_map/ppermute | solution.py:764
